TPU v7x, 32 devices: a whole 2x2x4 slice. The times are simulated.
32 devices in a mesh: groups: 2 (over y), ctx: 4 (over z), role: 2 (over x), seq: 2 (over core).
Axes of the slice: x: 2, y: 2, z: 4, core: 2. Of those that a mesh axis runs over, the one named last changes fastest.
Arguments:
- queries: bfloat16 [32, 128, 576], P(('groups', 'role', 'seq'), 'ctx'), parts along dimension 0, may hold values from -24 to 24
- cache: bfloat16 [16, 4096, 576], P(('groups', 'role', 'seq'), 'ctx'), parts along dimension 0, may hold values from -4 to 4
- lengths: int32 [16], P(('groups', 'role', 'seq')), parts along dimension 0, may hold values from 4 to 4096, as said below
- positions: int32 [32], P(('groups', 'role', 'seq')), parts along dimension 0, may hold values from 0 to 4098, as said below
- value_up_weight: bfloat16 [128, 512, 128], P('ctx', ('role', 'seq')), may hold values from -0.25 to 0.25
- out_proj: bfloat16 [16384, 7168], P('ctx', ('role', 'seq')), may hold values from -0.046875 to 0.046875
- residual: bfloat16 [32, 7168], P('groups', ('role', 'seq')), parts along dimension 0, may hold values from -4 to 4
- norm_gain: float32 [7168], P(('role', 'seq')), may hold values from 0.5 to 1.5
- gate_weight: bfloat16 [7168, 9216], P(('role', 'seq'), 'ctx'), may hold values from -0.0625 to 0.0625
- up_weight: bfloat16 [7168, 9216], P(('role', 'seq'), 'ctx'), may hold values from -0.0625 to 0.0625
- down_weight: bfloat16 [9216, 7168], P('ctx', ('role', 'seq')), may hold values from -0.0625 to 0.0625
Outputs:
- layer_out: bfloat16 [32, 7168], P(('groups', 'ctx'), ('role', 'seq')), parts along dimension 0
There are 2 independent parts, one for each index of `groups`. A program takes and returns all parts, laid end to end along the dimension named above; an argument that names none is the same for every part. Nothing has to cross between parts.
Inputs may be any that keep to these rules, and one draw needn't show every extreme that they name: `lengths`: every sequence has at least 4 cached positions, and in every draw some sequence has all 4096. positions[r] lies between lengths[r // 2] - 4 and lengths[r // 2] + 2.
All inputs are finite; a program needn't handle non-finite values.
Results may differ from a plain program's by a relative error of at most 0.013.
Values may be sent and summed in bfloat16 or wider, within the bound.
A program may use at most 128 MiB of HBM per device.

v0:
```python
import jax
import jax.numpy as jnp
from jax import lax
from jax.sharding import PartitionSpec as P

D = 7168
HEADS = 128
LATENT = 512
ROPE = 64
VDIM = 128
MTP = 2


softmax_scale = 0.07216878364870323
epsilon = 1e-06


def settle_heads(pieces):
    maxima, totals, partial_value = pieces
    highest = jnp.max(maxima, axis=0)
    factor = jnp.exp(maxima - highest[None])
    denom = jnp.sum(factor * totals, axis=0)
    numer = jnp.sum(factor[..., None] * partial_value, axis=0)
    return (numer / denom[..., None]).astype(jnp.bfloat16)


def per_device(
    queries,
    cache,
    lengths,
    positions,
    value_up_weight,
    out_proj,
    residual,
    norm_gain,
    gate_weight,
    up_weight,
    down_weight,
):
    all_heads = lax.all_gather(queries, "ctx", axis=1, tiled=True)
    heads_here = queries.shape[1]
    width = LATENT + ROPE
    context_local = cache.shape[1]
    seq_here = cache.shape[0]
    offset = lax.axis_index("ctx") * context_local
    places = offset + jnp.arange(context_local, dtype=jnp.int32)
    maxima_list = []
    totals_list = []
    partial_list = []
    for number in range(seq_here):
        rows_pair = all_heads[MTP * number : MTP * (number + 1)].reshape(MTP * HEADS, width)
        keys_here = cache[number]
        limits = jnp.repeat(positions[MTP * number : MTP * (number + 1)], HEADS)
        length = lengths[number]

        def compute_block(rows_pair=rows_pair, keys_here=keys_here, limits=limits, length=length):
            scores = (
                jnp.dot(rows_pair, keys_here.T, preferred_element_type=jnp.float32) * softmax_scale
            )
            live = (places[None, :] < length) & (places[None, :] <= limits[:, None])
            block_max = jnp.max(jnp.where(live, scores, jnp.float32(-1e30)), axis=-1)
            probs = jnp.exp(
                jnp.where(live, scores - block_max[:, None], jnp.float32(-1e30))
            ).astype(jnp.bfloat16)
            block_weight_sum = jnp.sum(probs.astype(jnp.float32), axis=-1)
            block_out = jnp.dot(probs, keys_here[:, :LATENT], preferred_element_type=jnp.float32)
            return (block_max, block_weight_sum, block_out)

        block_max, block_weight_sum, block_out = compute_block()
        maxima_list.append(block_max.reshape(MTP, HEADS))
        totals_list.append(block_weight_sum.reshape(MTP, HEADS))
        partial_list.append(block_out.reshape(MTP, HEADS, LATENT))
    maxima = jnp.concatenate(maxima_list, axis=0)
    totals = jnp.concatenate(totals_list, axis=0)
    partial_value = jnp.concatenate(partial_list, axis=0)
    attended_values = settle_heads(
        (
            lax.all_to_all(maxima[None], "ctx", split_axis=2, concat_axis=0, tiled=True),
            lax.all_to_all(totals[None], "ctx", split_axis=2, concat_axis=0, tiled=True),
            lax.all_to_all(partial_value[None], "ctx", split_axis=2, concat_axis=0, tiled=True),
        )
    )
    mixed = jnp.einsum(
        "nut,utc->nuc",
        attended_values,
        lax.all_gather(value_up_weight, ("role", "seq"), axis=1, tiled=True),
        preferred_element_type=jnp.float32,
    )
    value_vectors = mixed.astype(jnp.bfloat16).reshape(attended_values.shape[0], heads_here * VDIM)
    per_head_terms = jnp.dot(
        lax.all_gather(value_vectors, ("role", "seq"), axis=0, tiled=True),
        out_proj,
        preferred_element_type=jnp.float32,
    )
    attn_out = lax.psum(per_head_terms, "ctx")
    resid = residual.astype(jnp.float32) + attn_out
    sumsq = lax.psum(jnp.sum(resid * resid, axis=1), ("role", "seq"))
    normed = (resid * lax.rsqrt(sumsq / D + epsilon)[:, None] * norm_gain[None, :]).astype(
        jnp.bfloat16
    )
    gate_term = jnp.dot(normed, gate_weight, preferred_element_type=jnp.float32)
    up_term = jnp.dot(normed, up_weight, preferred_element_type=jnp.float32)
    gate, up = lax.psum((gate_term, up_term), ("role", "seq"))
    hidden = (jax.nn.silu(gate) * up).astype(jnp.bfloat16)
    rows_here = resid.shape[0] // lax.axis_size("ctx")
    ffn_rows = lax.psum_scatter(
        jnp.dot(hidden, down_weight, preferred_element_type=jnp.float32),
        "ctx",
        scatter_dimension=0,
        tiled=True,
    )
    base_rows = lax.dynamic_slice_in_dim(resid, lax.axis_index("ctx") * rows_here, rows_here, 0)
    return (base_rows + ffn_rows).astype(jnp.bfloat16)


def solution(mesh):
    placed = (
        P(("groups", "role", "seq"), "ctx", None),
        P(("groups", "role", "seq"), "ctx", None),
        P(("groups", "role", "seq")),
        P(("groups", "role", "seq")),
        P("ctx", ("role", "seq"), None),
        P("ctx", ("role", "seq")),
        P("groups", ("role", "seq")),
        P(("role", "seq")),
        P(("role", "seq"), "ctx"),
        P(("role", "seq"), "ctx"),
        P("ctx", ("role", "seq")),
    )
    return jax.shard_map(
        per_device,
        mesh=mesh,
        in_specs=placed,
        out_specs=P(("groups", "ctx"), ("role", "seq")),
        check_vma=False,
    )
```

profile of v0, /device:TPU:0, one launch (start us, length us, event | category | flops | bytes accessed | tf_op | source)
XLA Modules:
  0.0 227.1 jit_solution(11326140525146923370)
XLA Ops:
  6.5 0.7 all-gather.3.cloned.1.call-update
  7.3 1.3 fusion.19
  8.6 1.3 fusion.12
  9.9 19.9 %all_gather.9 = bf16[4,128,576]{2,1,0:T(8,128)(2,1)S(1)} all-gather(bf16[4,32,576]{2,1,0:T(8,128)(2,1)} %param.11), channel_id=1, replica_groups=mesh['groups'=2,'ctx'=4,'role'=2,'seq'=2] {'ctx'}, dimensions={1}, use_global_device_ids=true | all-gather | bytes 737280 | tf_op jit(solution)/shard_map/all_gather | solution.py:40
  29.8 0.8 fusion.20
  30.7 1.8 convolution_multiply_fusion
  32.6 0.9 select_reduce_fusion.1
  33.5 0.9 convert_reduce_fusion.1
  34.4 0.1 copy.23
  34.5 0.6 broadcast.49
  35.1 0.8 reduce.1
  35.9 0.7 reshape.68
  36.6 3.8 %all-to-all-start.2 = ((f32[4,1,128]{2,1,0:T(1,128)}), f32[4,1,128]{2,1,0:T(1,128)S(1)}, u32[]{:S(2)}, u32[]{:S(2)}) async-start(f32[4,1,128]{2,1,0:T(1,128)} %reshape.68), calls=%async_computation.2 | async-start | bytes 4096 | tf_op jit(solution)/shard_map/all_to_all | solution.py:79
  40.4 0.2 slice_bitcast_fusion.1
  40.6 0.5 fusion.3
  41.1 0.5 fusion.1
  41.6 0.1 copy.18
  41.7 0.8 reduce.3
  42.5 0.7 reshape.66
  43.2 0.4 copy.20
  43.6 0.4 copy.21
  44.0 1.9 all-to-all-done.2
  45.9 3.2 %all-to-all-start = ((f32[4,1,128]{2,1,0:T(1,128)}), f32[4,1,128]{2,1,0:T(1,128)S(1)}, u32[]{:S(2)}, u32[]{:S(2)}) async-start(f32[4,1,128]{2,1,0:T(1,128)} %reshape.66), calls=%async_computation | async-start | bytes 4096 | tf_op jit(solution)/shard_map/all_to_all | solution.py:78
  49.1 1.4 maximum_bitcast_fusion
  50.6 4.1 %all-to-all-done = f32[4,1,128]{2,1,0:T(1,128)S(1)} async-done(((f32[4,1,128]{2,1,0:T(1,128)}), f32[4,1,128]{2,1,0:T(1,128)S(1)}, u32[]{:S(2)}, u32[]{:S(2)}) %all-to-all-start) | async-done | bytes 2080 | tf_op jit(solution)/shard_map/all_to_all | solution.py:78
  54.7 3.5 %all-to-all-start.1 = ((f32[1,4,128,512]{3,1,0,2:T(4,128)}), f32[1,4,128,512]{3,1,0,2:T(4,128)S(1)}, u32[]{:S(2)}, u32[]{:S(2)}) async-start(f32[1,4,128,512]{3,1,0,2:T(4,128)} %maximum_bitcast_fusion), calls=%async_computation.1 | async-start | bytes 2097152 | tf_op jit(solution)/shard_map/all_to_all | solution.py:80
  58.3 0.7 reduce.2
  58.9 0.1 reshape.69
  59.1 0.1 copy.24
  59.2 0.7 reduce.4
  59.8 0.1 reshape.67
  60.0 0.1 copy.19
  60.1 18.8 %all-to-all-done.1 = f32[1,4,128,512]{3,1,0,2:T(4,128)S(1)} async-done(((f32[1,4,128,512]{3,1,0,2:T(4,128)}), f32[1,4,128,512]{3,1,0,2:T(4,128)S(1)}, u32[]{:S(2)}, u32[]{:S(2)}) %all-to-all-start.1) | async-done | bytes 1048608 | tf_op jit(solution)/shard_map/all_to_all | solution.py:80
  78.9 0.3 fusion.5
  79.3 0.1 divide_convert_fusion
  79.4 2.8 %fusion = bf16[1,4,4096]{2,1,0:T(4,128)(2,1)S(1)} fusion(bf16[32,512,128]{2,1,0:T(8,128)(2,1)} %all-gather.3.cloned.1.call-done, bf16[4,32,512]{2,1,0:T(8,128)(2,1)S(1)} %divide_convert_fusion), kind=kOutput, calls=%fused_computation.5 | convolution fusion | flops 16793600 | bytes 4358144 | tf_op jit(solution)/shard_map/nut,utc->nuc/dot_general | solution.py:83
  82.2 5.4 %all-gather = bf16[4,4,4096]{2,1,0:T(4,128)(2,1)S(1)} all-gather(bf16[1,4,4096]{2,1,0:T(4,128)(2,1)S(1)} %fusion), channel_id=1, replica_groups=mesh['groups'=2,'ctx'=4,'role'=2,'seq'=2] {'role','seq'}, dimensions={0}, use_global_device_ids=true | all-gather | bytes 163840 | tf_op jit(solution)/shard_map/all_gather | solution.py:91
  87.7 7.8 %fusion.21 = f32[16,1792]{1,0:T(8,128)} fusion(bf16[16,4096]{1,0:T(8,128)(2,1)S(1)} %reshape.63, bf16[4096,1792]{1,0:T(8,128)(2,1)} %param.16), kind=kOutput, calls=%fused_computation.50 | convolution fusion | flops 234881024 | bytes 14925824 | tf_op jit(solution)/shard_map/dot_general | solution.py:90
  95.6 33.5 %all-reduce.6.cloned.1.call-done = f32[16,1792]{1,0:T(8,128)} async-done(((f32[16,1792]{1,0:T(8,128)}), f32[16,1792]{1,0:T(8,128)}) %all-reduce.6.cloned.1.call-update) | async-done | bytes 114704 | tf_op jit(solution)/shard_map/psum | solution.py:95
  129.1 1.0 multiply_reduce_fusion
  130.1 5.7 %psum.29 = f32[16]{0:T(128)S(1)} all-reduce(f32[16]{0:T(128)S(1)} %get-tuple-element.9), channel_id=1, replica_groups=mesh['groups'=2,'ctx'=4,'role'=2,'seq'=2] {'role','seq'}, use_global_device_ids=true, to_apply=%region_9.10 | all-reduce | flops 16 | bytes 128 | tf_op jit(solution)/shard_map/psum | solution.py:97
  135.8 5.2 %fusion.16 = f32[16,2304]{1,0:T(8,128)} fusion(bf16[1792,2304]{1,0:T(8,128)(2,1)} %param.19, f32[16,1792]{1,0:T(8,128)S(1)} %get-tuple-element.10, f32[1792]{0:T(1024)S(1)} %copy-done.1, f32[16]{0:T(128)S(1)} %add_rsqrt_fusion), kind=kOutput, calls=%fused_computation.46 | convolution fusion | flops 132206592 | bytes 8526912 | tf_op jit(solution)/shard_map/dot_general | solution.py:101
  141.1 5.3 %fusion.15 = f32[16,2304]{1,0:T(8,128)} fusion(bf16[1792,2304]{1,0:T(8,128)(2,1)} %param.20, f32[16,1792]{1,0:T(8,128)S(1)} %get-tuple-element.10, f32[1792]{0:T(1024)S(1)} %copy-done.1, f32[16]{0:T(128)S(1)} %add_rsqrt_fusion), kind=kOutput, calls=%fused_computation.45 | convolution fusion | flops 132206592 | bytes 8526912 | tf_op jit(solution)/shard_map/dot_general | solution.py:102
  146.4 32.9 %all-reduce.10.cloned.1.call-done = (f32[16,2304]{1,0:T(8,128)}, f32[16,2304]{1,0:T(8,128)}) async-done(((f32[16,2304]{1,0:T(8,128)}, f32[16,2304]{1,0:T(8,128)}), (f32[16,2304]{1,0:T(8,128)}, f32[16,2304]{1,0:T(8,128)})) %all-reduce.10.cloned.1.call-update) | async-done | bytes 294928 | tf_op jit(solution)/shard_map/psum | solution.py:103
  179.2 5.4 %fusion.7 = f32[16,1792]{1,0:T(8,128)} fusion(bf16[2304,1792]{1,0:T(8,128)(2,1)} %param.21, f32[16,2304]{1,0:T(8,128)} %get-tuple-element.7, f32[16,2304]{1,0:T(8,128)} %get-tuple-element.8), kind=kOutput, calls=%fused_computation.27 | convolution fusion | flops 132341760 | bytes 8667136 | tf_op jit(solution)/shard_map/dot_general | solution.py:107
  184.7 0.6 dynamic-slice
  185.9 33.3 %all-reduce.8.cloned.1.call-done = f32[16,1792]{1,0:T(8,128)} async-done(((f32[16,1792]{1,0:T(8,128)}), f32[16,1792]{1,0:T(8,128)}) %all-reduce.8.cloned.1.call-update) | async-done | bytes 114704
  219.2 1.4 fusion.9
  (25 shorter events, 0.5 us)
Async XLA Ops:
  6.5 26.1 %copy-start = (bf16[2,1024,576]{1,2,0:T(8,128)(2,1)S(1)}, bf16[2,1024,576]{1,2,0:T(8,128)(2,1)}, u32[]{:S(2)}) copy-start(bf16[2,1024,576]{1,2,0:T(8,128)(2,1)} %param.12) | copy-start | bytes 7077892
  6.5 72.8 %all-gather.3.cloned.1.call-start = ((), (), s32[]{:S(2)}) async-start(), calls=%async_computation.3 | async-start | bytes 5242880 | tf_op jit(solution)/shard_map/all_gather | solution.py:86
  36.6 9.3 %all-to-all-start.2 = ((f32[4,1,128]{2,1,0:T(1,128)}), f32[4,1,128]{2,1,0:T(1,128)S(1)}, u32[]{:S(2)}, u32[]{:S(2)}) async-start(f32[4,1,128]{2,1,0:T(1,128)} %reshape.68), calls=%async_computation.2 | async-start | bytes 4096 | tf_op jit(solution)/shard_map/all_to_all | solution.py:79
  45.9 8.8 %all-to-all-start = ((f32[4,1,128]{2,1,0:T(1,128)}), f32[4,1,128]{2,1,0:T(1,128)S(1)}, u32[]{:S(2)}, u32[]{:S(2)}) async-start(f32[4,1,128]{2,1,0:T(1,128)} %reshape.66), calls=%async_computation | async-start | bytes 4096 | tf_op jit(solution)/shard_map/all_to_all | solution.py:78
  54.7 24.2 %all-to-all-start.1 = ((f32[1,4,128,512]{3,1,0,2:T(4,128)}), f32[1,4,128,512]{3,1,0,2:T(4,128)S(1)}, u32[]{:S(2)}, u32[]{:S(2)}) async-start(f32[1,4,128,512]{3,1,0,2:T(4,128)} %maximum_bitcast_fusion), calls=%async_computation.1 | async-start | bytes 2097152 | tf_op jit(solution)/shard_map/all_to_all | solution.py:80
  58.2 70.9 %all-reduce.6.cloned.1.call-start = ((), (), s32[]{:S(2)}) async-start(), calls=%async_computation.4 | async-start | bytes 229376 | tf_op jit(solution)/shard_map/psum | solution.py:95
  87.7 41.4 %copy-start.2 = (bf16[16,1792]{1,0:T(8,128)(2,1)S(1)}, bf16[16,1792]{1,0:T(8,128)(2,1)}, u32[]{:S(2)}) copy-start(bf16[16,1792]{1,0:T(8,128)(2,1)} %param.17) | copy-start | bytes 172036
  87.7 48.1 %copy-start.1 = (f32[1792]{0:T(1024)S(1)}, f32[1792]{0:T(1024)}, u32[]{:S(2)}) copy-start(f32[1792]{0:T(1024)} %param.18) | copy-start | bytes 21508
  95.6 83.7 %all-reduce.10.cloned.1.call-start = ((), (), s32[]{:S(2)}) async-start(), calls=%async_computation.6 | async-start | bytes 589824 | tf_op jit(solution)/shard_map/psum | solution.py:103
  146.3 72.8 %all-reduce.8.cloned.1.call-start = ((), (), s32[]{:S(2)}) async-start(), calls=%async_computation.5 | async-start | bytes 229376
  179.2 5.4 %copy-start.3 = (u32[32]{0:T(128)S(1)}, u32[32]{0:T(128)}, u32[]{:S(2)}) copy-start(u32[32]{0:T(128)} %constant.35) | copy-start | bytes 388
Sparse Core Ops, SparseCore 0:
  8.9 37.1 all-gather.2
  95.7 33.3 all-reduce.5
  146.4 32.7 all-reduce.9
  184.8 34.3 all-reduce.7
where the time goes:
time: 228 us; the launch traced here: 227 us
  waiting for transfers between devices  125 us (55%)
  blocking collectives  31 us (14%)
  matrix products  30.3 us (13%)
  between operations  14 us (6%)
  starting transfers between devices  10.7 us (5%)
  other arithmetic  9.47 us (4%)
  local copies, waits for them, and re-layouts  6.56 us (3%)
    unnamed x5, waiting for transfers between devices  34 us
    psum x1, waiting for transfers between devices, per_device(): attn_out = lax.psum(per_head_terms, 'ctx')  33.5 us
    psum x1, waiting for transfers between devices, per_device(): gate, up = lax.psum((gate_term, up_term), ('role', 'seq'))  32.9 us
    all_gather x1, blocking collectives, per_device(): all_heads = lax.all_gather(queries, 'ctx', axis=1, tiled=True)  19.9 us
    all_to_all x1, waiting for transfers between devices, per_device(): lax.all_to_all(partial_value[None], 'ctx', split_axis=2, concat_axis=0, t...  18.8 us
    dot_general x1, matrix products, per_device(): jnp.dot(lax.all_gather(value_vectors, ('role', 'seq'), axis=0, tiled=True...  7.84 us
    psum x1, blocking collectives, per_device(): sumsq = lax.psum(jnp.sum(resid * resid, axis=1), ('role', 'seq'))  5.66 us
    all_gather x1, blocking collectives, per_device(): lax.all_gather(value_vectors, ('role', 'seq'), axis=0, tiled=True)  5.41 us
  transfers between devices with their start and end apart: 7, of which 6 were waited for; matrix products, arithmetic and copies ran while one was open for 8% of the time, Pallas kernels for 0%

commit v1 on v0

v1 whole, which is shorter than its diff:
```python
import functools

import jax
import jax.numpy as jnp
from jax import lax
from jax.experimental import pallas as pl
from jax.experimental.pallas import tpu as pltpu
from jax.sharding import PartitionSpec as P

D = 7168
LATENT = 512
MTP = 2

softmax_scale = 0.07216878364870323
epsilon = 1e-06
MESH = pl.DeviceIdType.MESH
VMEM_BYTES = 60 * 1024 * 1024
f32, bf16 = jnp.float32, jnp.bfloat16


def ctx_group(n):
    me = lax.axis_index("ctx")

    def peer(d):
        k = lax.rem(me + d, n)
        return k, {"ctx": k}

    return me, peer


def feature_group(n_role, n_seq):
    n = n_role * n_seq
    me = lax.axis_index("role") * n_seq + lax.axis_index("seq")

    def peer(d):
        k = lax.rem(me + d, n)
        return k, {"role": k // n_seq, "seq": lax.rem(k, n_seq)}

    return me, peer


def enter(groups):
    barrier = pltpu.get_barrier_semaphore()
    count = 0
    for n, peer in groups:
        for d in range(1, n):
            pl.semaphore_signal(barrier, inc=1, device_id=peer(d)[1], device_id_type=MESH)
            count += 1
    pl.semaphore_wait(barrier, count)


def remote(src, dst, send, recv, device):
    return pltpu.make_async_remote_copy(
        src_ref=src, dst_ref=dst, send_sem=send, recv_sem=recv,
        device_id=device, device_id_type=MESH,
    )


def attend_kernel(n, n_role, n_seq, q_ref, cache_ref, len_ref, pos_ref, out_ref,
                  q_all, o_send, o_recv, s_send, s_recv, a_send, sems):
    nr = n_role * n_seq
    me, peer = ctx_group(n)
    fme, fpeer = feature_group(n_role, n_seq)
    enter(((n, peer), (nr, fpeer)))
    seqs, context, _ = cache_ref.shape
    rows = q_ref.shape[0] // seqs
    heads = rows // MTP

    q_copies = []
    for d in range(1, n):
        c = remote(q_ref, q_all.at[me], sems.at[0, d], sems.at[1, d], peer(d)[1])
        c.start()
        q_copies.append(c)

    places = me * context + lax.broadcasted_iota(jnp.int32, (rows, context), 1)
    first = lax.broadcasted_iota(jnp.int32, (rows, context), 0) < heads
    lives = []
    for s in range(seqs):
        limit = jnp.where(first, pos_ref[MTP * s], pos_ref[MTP * s + 1])
        lives.append((places < len_ref[s]) & (places <= limit))

    def block(q):
        outs, stats = [], []
        for s in range(seqs):
            keys = cache_ref[s]
            scores = lax.dot_general(
                q[s * rows:(s + 1) * rows], keys, (((1,), (1,)), ((), ())),
                preferred_element_type=f32) * softmax_scale
            live = lives[s]
            top = jnp.max(jnp.where(live, scores, -1e30), axis=1, keepdims=True)
            probs = jnp.exp(jnp.where(live, scores - top, -1e30)).astype(bf16)
            total = jnp.sum(probs.astype(f32), axis=1, keepdims=True)
            outs.append(jnp.dot(probs, keys[:, :LATENT], preferred_element_type=f32))
            lane = lax.broadcasted_iota(jnp.int32, (rows, 128), 1)
            stats.append(jnp.where(lane == 0, top, total))
        return jnp.concatenate(outs, axis=0), jnp.concatenate(stats, axis=0)

    own_o, own_s = block(q_ref[...])
    o_copies, s_copies = [], []
    for d in range(1, n):
        src, device = peer(n - d)
        remote(q_all.at[src], q_all.at[src], sems.at[0, d], sems.at[1, d], device).wait_recv()
        o, s = block(q_all[src])
        o_send[d] = o.astype(bf16)
        s_send[d] = s.T[0:8]
        c = remote(o_send.at[d], o_recv.at[d], sems.at[2, d], sems.at[3, d], device)
        c.start()
        o_copies.append(c)
        c = remote(s_send.at[d], s_recv.at[d], sems.at[4, d], sems.at[5, d], device)
        c.start()
        s_copies.append(c)
    for c in q_copies:
        c.wait_send()

    all_rows = q_ref.shape[0]
    tops, totals = [own_s[:, 0:1]], [own_s[:, 1:2]]
    for d in range(1, n):
        s_copies[d - 1].wait()
        back = jnp.concatenate([s_recv[d]] * 16, axis=0).T
        tops.append(back[:, 0:1])
        totals.append(back[:, 1:2])
    highest = functools.reduce(jnp.maximum, tops)
    factors = [jnp.exp(t - highest) for t in tops]
    denom = sum(f * t for f, t in zip(factors, totals))
    numer = factors[0] * own_o
    for d in range(1, n):
        o_copies[d - 1].wait()
        numer = numer + factors[d] * o_recv[d].astype(f32)
    attended = (numer / denom).astype(bf16)

    part = LATENT // nr
    for k in range(nr):
        a_send[k] = attended[:, k * part:(k + 1) * part]
    copies = []
    for d in range(1, nr):
        k, device = fpeer(d)
        c = remote(a_send.at[k], out_ref.at[fme], sems.at[6, d], sems.at[7, d], device)
        c.start()
        copies.append(c)
    out_ref[fme] = a_send[fme]
    for d in range(1, nr):
        k, device = fpeer(nr - d)
        copies[d - 1].wait_send()
        remote(a_send.at[k], out_ref.at[k], sems.at[6, d], sems.at[7, d], device).wait_recv()


def layer_kernel(n, n_role, n_seq, pv_ref, res_ref, gain_ref, wo_hbm, wg_hbm, wu_hbm, wd_hbm,
                 out_ref, wo, wg, wu, wd, pv_recv, v_send, v_all, v_full, acc, po_send, po_recv,
                 resid, xg_ref, g_acc, u_acc, gu_send, gu_recv, ss_send, ss_recv, h_send, h_all,
                 h_full, dn, dn_send, dn_recv, wsem, sems):
    nr = n_role * n_seq
    me, peer = ctx_group(n)
    fme, fpeer = feature_group(n_role, n_seq)

    weights = []
    for which, (hbm, vmem) in enumerate(((wo_hbm, wo), (wg_hbm, wg), (wu_hbm, wu), (wd_hbm, wd))):
        depth = vmem.shape[1]

        def fetch(i, hbm=hbm, vmem=vmem, depth=depth, which=which):
            return pltpu.make_async_copy(
                hbm.at[pl.ds(i * depth, depth)], vmem.at[i], wsem.at[which, i])

        weights.append((fetch, vmem))
    for fetch, vmem in weights:
        for i in range(vmem.shape[0]):
            fetch(i).start()
    enter(((n, peer), (nr, fpeer)))

    def matmul(x_ref, which, acc_ref):
        fetch, vmem = weights[which]
        depth = vmem.shape[1]
        acc_ref[...] = jnp.zeros_like(acc_ref)
        if vmem.shape[0] == 1:
            fetch(0).wait()
            acc_ref[...] = jnp.dot(x_ref[...], vmem[0], preferred_element_type=f32)
            return

        @pl.loop(0, vmem.shape[0])
        def _(i):
            fetch(i).wait()
            x = x_ref[:, pl.ds(pl.multiple_of(i * depth, depth), depth)]
            acc_ref[...] += jnp.dot(x, vmem[i], preferred_element_type=f32)

    def swap(size, peer_of, chunk, recv, row):
        copies = []
        for d in range(1, size):
            k, device = peer_of(d)
            c = remote(chunk(k), recv.at[d], sems.at[row, d], sems.at[row + 1, d], device)
            c.start()
            copies.append(c)
        return copies

    def gather(size, my, peer_of, send, full, row):
        copies = []
        for d in range(1, size):
            c = remote(send, full.at[my], sems.at[row, d], sems.at[row + 1, d], peer_of(d)[1])
            c.start()
            copies.append(c)
        full[my] = send[...]
        for d in range(1, size):
            k, device = peer_of(size - d)
            copies[d - 1].wait_send()
            remote(send, full.at[k], sems.at[row, d], sems.at[row + 1, d], device).wait_recv()

    part = res_ref.shape[0] // nr
    copies = swap(nr, fpeer, lambda k: pv_ref.at[k], pv_recv, 0)
    vals = pv_ref[fme].astype(f32)
    for d in range(1, nr):
        copies[d - 1].wait()
        vals = vals + pv_recv[d].astype(f32)
    v_send[...] = vals.astype(bf16)
    gather(nr, fme, fpeer, v_send, v_all, 2)
    for k in range(nr):
        acc_rows = v_all[k].astype(f32)
        v_full[k * part:(k + 1) * part, :] = acc_rows
    x_ref = xg_ref[0]
    x_ref[...] = v_full[...].astype(bf16)
    matmul(x_ref, 0, acc)

    po_send[...] = acc[...].astype(bf16)
    copies = swap(n, peer, lambda k: po_send, po_recv, 4)
    total = res_ref[...].astype(f32) + acc[...]
    for d in range(1, n):
        copies[d - 1].wait()
        total = total + po_recv[d].astype(f32)
    crows = res_ref.shape[0] // n
    for k in range(n):
        resid[k] = total[k * crows:(k + 1) * crows]
    sumsq = jnp.sum(total * total, axis=1, keepdims=True)
    sumsq = jnp.broadcast_to(sumsq, (total.shape[0], 128))
    for k in range(nr):
        ss_send[k] = sumsq[k * part:(k + 1) * part]
    s_copies = swap(nr, fpeer, lambda k: ss_send.at[k], ss_recv, 6)
    x_ref = xg_ref[1]
    x_ref[...] = (total * gain_ref[...]).astype(bf16)
    matmul(x_ref, 1, g_acc)
    matmul(x_ref, 2, u_acc)

    for j, a in enumerate((g_acc, u_acc)):
        for k in range(nr):
            gu_send[k, j] = a[k * part:(k + 1) * part, :].astype(bf16)
    copies = swap(nr, fpeer, lambda k: gu_send.at[k], gu_recv, 8)
    ss = ss_send[fme]
    for d in range(1, nr):
        s_copies[d - 1].wait()
        ss = ss + ss_recv[d]
    inv = lax.rsqrt(ss[:, 0:1] / D + epsilon)
    gate = gu_send[fme, 0].astype(f32)
    up = gu_send[fme, 1].astype(f32)
    for d in range(1, nr):
        copies[d - 1].wait()
        gate = gate + gu_recv[d, 0].astype(f32)
        up = up + gu_recv[d, 1].astype(f32)
    gate = gate * inv
    up = up * inv
    h_send[...] = (gate / (1.0 + jnp.exp(-gate)) * up).astype(bf16)
    gather(nr, fme, fpeer, h_send, h_all, 10)
    for k in range(nr):
        h_full[k * part:(k + 1) * part, :] = h_all[k].astype(f32)
    x_ref = xg_ref[2]
    x_ref[...] = h_full[...].astype(bf16)
    matmul(x_ref, 3, acc)

    for k in range(n):
        piece = acc[k * crows:(k + 1) * crows, :]
        dn[k] = piece
        dn_send[k] = piece.astype(bf16)
    copies = swap(n, peer, lambda k: dn_send.at[k], dn_recv, 12)
    result = resid[me] + dn[me]
    for d in range(1, n):
        copies[d - 1].wait()
        result = result + dn_recv[d].astype(f32)
    out_ref[...] = result.astype(bf16)


def chunk_of(depth):
    for size in (512, 256):
        if depth % size == 0:
            return size
    return depth


def per_device(sizes, queries, cache, lengths, positions, value_up_weight, out_proj, residual,
               norm_gain, gate_weight, up_weight, down_weight):
    n, n_role, n_seq = sizes
    nr = n_role * n_seq
    rows, heads, width = queries.shape
    flat = rows * heads
    lat = LATENT // nr
    vmem = pl.BlockSpec(memory_space=pltpu.VMEM)
    smem = pl.BlockSpec(memory_space=pltpu.SMEM)
    hbm = pl.BlockSpec(memory_space=pl.ANY)
    most = max(n, nr)
    sems = lambda k: pltpu.SemaphoreType.DMA((k, most))
    attended = pl.pallas_call(
        functools.partial(attend_kernel, n, n_role, n_seq),
        out_shape=jax.ShapeDtypeStruct((nr, flat, lat), bf16),
        in_specs=[vmem, vmem, smem, smem],
        out_specs=vmem,
        scratch_shapes=[
            pltpu.VMEM((n, flat, width), bf16),
            pltpu.VMEM((n, flat, LATENT), bf16),
            pltpu.VMEM((n, flat, LATENT), bf16),
            pltpu.VMEM((n, 8, flat), f32),
            pltpu.VMEM((n, 8, flat), f32),
            pltpu.VMEM((nr, flat, lat), bf16),
            sems(8),
        ],
        compiler_params=pltpu.CompilerParams(
            collective_id=0, has_side_effects=True, vmem_limit_bytes=VMEM_BYTES),
        name="attend",
    )(queries.reshape(flat, width), cache, lengths, positions)
    by_head = attended.reshape(nr, rows, heads, lat).transpose(2, 0, 1, 3).reshape(heads, nr * rows, lat)
    mixed = jnp.einsum("hrk,hkv->rhv", by_head, value_up_weight, preferred_element_type=f32)
    vwide = heads * value_up_weight.shape[2]
    pv = mixed.astype(bf16).reshape(nr, rows, vwide)

    all_rows, dd = residual.shape
    ff = gate_weight.shape[1]
    part, crows = all_rows // nr, all_rows // n

    def held(w):
        size = chunk_of(w.shape[0])
        return pltpu.VMEM((w.shape[0] // size, size, w.shape[1]), bf16)

    ws = (out_proj, gate_weight, up_weight, down_weight)
    most_chunks = max(w.shape[0] // chunk_of(w.shape[0]) for w in ws)
    V = pltpu.VMEM
    return pl.pallas_call(
        functools.partial(layer_kernel, n, n_role, n_seq),
        out_shape=jax.ShapeDtypeStruct((crows, dd), bf16),
        in_specs=[vmem] * 3 + [hbm] * 4,
        out_specs=vmem,
        scratch_shapes=[
            *[held(w) for w in ws],
            V((nr, part, vwide), bf16),
            V((part, vwide), bf16),
            V((nr, part, vwide), bf16),
            V((all_rows, vwide), f32),
            V((all_rows, dd), f32),
            V((all_rows, dd), bf16),
            V((n, all_rows, dd), bf16),
            V((n, crows, dd), f32),
            [V((all_rows, vwide), bf16), V((all_rows, dd), bf16), V((all_rows, ff), bf16)],
            V((all_rows, ff), f32),
            V((all_rows, ff), f32),
            V((nr, 2, part, ff), bf16),
            V((nr, 2, part, ff), bf16),
            V((nr, part, 128), f32),
            V((nr, part, 128), f32),
            V((part, ff), bf16),
            V((nr, part, ff), bf16),
            V((all_rows, ff), f32),
            V((n, crows, dd), f32),
            V((n, crows, dd), bf16),
            V((n, crows, dd), bf16),
            pltpu.SemaphoreType.DMA((4, most_chunks)),
            sems(14),
        ],
        compiler_params=pltpu.CompilerParams(
            collective_id=1, has_side_effects=True, vmem_limit_bytes=VMEM_BYTES),
        name="layer",
    )(pv, residual, norm_gain.reshape(1, dd), *ws)


def solution(mesh):
    placed = (
        P(("groups", "role", "seq"), "ctx", None),
        P(("groups", "role", "seq"), "ctx", None),
        P(("groups", "role", "seq")),
        P(("groups", "role", "seq")),
        P("ctx", ("role", "seq"), None),
        P("ctx", ("role", "seq")),
        P("groups", ("role", "seq")),
        P(("role", "seq")),
        P(("role", "seq"), "ctx"),
        P(("role", "seq"), "ctx"),
        P("ctx", ("role", "seq")),
    )
    sizes = (mesh.shape["ctx"], mesh.shape["role"], mesh.shape["seq"])
    return jax.shard_map(
        functools.partial(per_device, sizes),
        mesh=mesh,
        in_specs=placed,
        out_specs=P(("groups", "ctx"), ("role", "seq")),
        check_vma=False,
    )
```

time: 228 us -> 86.7 us (0.38)
  waiting for transfers between devices: 125 us -> 0 us
  Pallas kernels: 0 us -> 78 us
  blocking collectives: 31 us -> 0 us
  matrix products: 30.3 us -> 0.37 us
  between operations: 14 us -> 0.04 us
  starting transfers between devices: 10.7 us -> 0 us
  other arithmetic: 9.47 us -> 0 us
    pallas_call x0 -> x2, Pallas kernels: none -> 78 us  [the longest x1 42.3 us: per_device(): pl.pallas_call(functools.partial(attend_kernel, n, n_role, n_seq), out_sh...]
    psum x2 -> x0, waiting for transfers between devices: 66.4 us -> none  [the longest x1 33.5 us: per_device(): attn_out = lax.psum(per_head_terms, 'ctx')]
    unnamed x5 -> x0, waiting for transfers between devices: 34 us -> none
    dot_general x9 -> x1, matrix products: 30.3 us -> 0.37 us  [per_device(): jnp.einsum('hrk,hkv->rhv', by_head, value_up_weight, preferred_element_ty...]
    all_gather x2 -> x0, blocking collectives: 25.3 us -> none  [the longest x1 19.9 us: per_device(): all_heads = lax.all_gather(queries, 'ctx', axis=1, tiled=True)]
    all_to_all x3 -> x0, waiting for transfers between devices: 24.8 us -> none  [the longest x1 18.8 us: per_device(): lax.all_to_all(partial_value[None], 'ctx', split_axis=2, concat_axis=0, t...]
    all_to_all x3 -> x0, starting transfers between devices: 10.5 us -> none  [the longest x1 3.8 us: per_device(): lax.all_to_all(totals[None], 'ctx', split_axis=2, concat_axis=0, tiled=True)]
    psum x1 -> x0, blocking collectives: 5.66 us -> none  [per_device(): sumsq = lax.psum(jnp.sum(resid * resid, axis=1), ('role', 'seq'))]
  transfers between devices with their start and end apart: 7 -> 0, of which waited for: 6 -> 0; matrix products, arithmetic and copies ran while one was open for 8% -> 0% of each run, Pallas kernels for 0% -> 0%
where the time goes in v1:
time: 86.7 us; the launch traced here: 86.4 us
  Pallas kernels  78 us (90%)
  local copies, waits for them, and re-layouts  8.04 us (9%)
    pallas_call x1, Pallas kernels, per_device(): pl.pallas_call(functools.partial(attend_kernel, n, n_role, n_seq), out_sh...  42.3 us
    pallas_call x1, Pallas kernels, per_device(): pl.pallas_call(functools.partial(layer_kernel, n, n_role, n_seq), out_sha...  35.6 us
    unnamed x6, local copies, waits for them, and re-layouts  5.74 us

profile of v1, /device:TPU:0, one launch (start us, length us, event | category | flops | bytes accessed | tf_op | source)
XLA Modules:
  0.0 86.4 jit_solution(9400615228546427837)
XLA Ops:
  0.0 0.0 copy-start
  0.0 0.0 copy-start.1
  0.0 4.4 %copy.12.cache_ref = bf16[2,1024,576]{2,1,0:T(8,128)(2,1)} copy(bf16[2,1024,576]{1,2,0:T(8,128)(2,1)} %param.12) | data formatting | bytes 4718592 | tf_op args[1]
  4.4 42.3 %attend.1 = bf16[4,128,128]{2,1,0:T(8,128)(2,1)} custom-call(bf16[128,576]{1,0:T(8,128)(2,1)} %bitcast.11, bf16[2,1024,576]{2,1,0:T(8,128)(2,1)} %copy.12.cache_ref, s32[2]{0:T(128)} %len_ref.1, s32[4]{0:T(128)} %pos_ref.1), custom_call_target="tpu_custom_call" | custom-call | tf_op jit(solution)/shard_map/attend/pallas_call | solution.py:295
  46.8 1.0 %copy.13 = bf16[32,4,4,128]{3,2,1,0:T(4,128)(2,1)S(1)} copy(bf16[32,4,4,128]{3,0,2,1:T(8,128)(2,1)} %bitcast.10) | data formatting | bytes 262144 | tf_op jit(solution)/shard_map/transpose | solution.py:313
  47.7 0.0 copy-done
  47.7 0.4 fusion
  48.1 0.1 copy.14
  48.2 0.7 reshape.18.pv_ref
  48.8 0.0 copy-done.1
  48.8 0.6 reshape.19.gain_ref
  49.4 35.6 %layer.1 = bf16[4,1792]{1,0:T(4,128)(2,1)} custom-call(bf16[4,4,4096]{2,1,0:T(4,128)(2,1)} %reshape.18.pv_ref, bf16[16,1792]{1,0:T(8,128)(2,1)} %res_ref.1, f32[1,1792]{1,0:T(1,128)} %reshape.19.gain_ref, bf16[4096,1792]{1,0:T(8,128)(2,1)} %wo_hbm.1, bf16[1792,2304]{1,0:T(8,128)(2,1)} %wg_hbm.1, bf16[1792,2304]{1,0:T(8,128)(2,1)} %wu_hbm.1, ...), custom_call_target="tpu_custom_call" | custom-call | tf_op jit(solution)/shard_map/layer/pallas_call | solution.py:329
  85.1 1.3 %copy.16 = bf16[4,1792]{1,0:T(4,128)(2,1)} copy(bf16[4,1792]{1,0:T(4,128)(2,1)} %layer.1) | data formatting | bytes 28672
Async XLA Ops:
  0.0 47.7 %copy-start = (bf16[32,128,128]{2,1,0:T(8,128)(2,1)S(1)}, bf16[32,128,128]{2,1,0:T(8,128)(2,1)}, u32[]{:S(2)}) copy-start(bf16[32,128,128]{2,1,0:T(8,128)(2,1)} %param.15) | copy-start | bytes 3145732
  0.0 48.8 %copy-start.1 = (f32[1792]{0:T(1024)S(1)}, f32[1792]{0:T(1024)}, u32[]{:S(2)}) copy-start(f32[1792]{0:T(1024)} %param.18) | copy-start | bytes 21508

commit v2 on v1

--- a/solution.py
+++ b/solution.py
@@ -56,13 +56,12 @@
     )
 
 
-def attend_kernel(n, n_role, n_seq, q_ref, cache_ref, len_ref, pos_ref, out_ref,
-                  q_all, o_send, o_recv, s_send, s_recv, a_send, sems):
+def attend(n, n_role, n_seq, q_ref, cache_ref, cache_copy, len_ref, pos_ref, out_ref,
+           q_all, o_send, o_recv, s_send, s_recv, a_send, sems):
     nr = n_role * n_seq
     me, peer = ctx_group(n)
     fme, fpeer = feature_group(n_role, n_seq)
-    enter(((n, peer), (nr, fpeer)))
-    seqs, context, _ = cache_ref.shape
+    seqs, _, context = cache_ref.shape
     rows = q_ref.shape[0] // seqs
     heads = rows // MTP
 
@@ -84,17 +83,19 @@
         for s in range(seqs):
             keys = cache_ref[s]
             scores = lax.dot_general(
-                q[s * rows:(s + 1) * rows], keys, (((1,), (1,)), ((), ())),
+                q[s * rows:(s + 1) * rows], keys, (((1,), (0,)), ((), ())),
                 preferred_element_type=f32) * softmax_scale
             live = lives[s]
             top = jnp.max(jnp.where(live, scores, -1e30), axis=1, keepdims=True)
             probs = jnp.exp(jnp.where(live, scores - top, -1e30)).astype(bf16)
             total = jnp.sum(probs.astype(f32), axis=1, keepdims=True)
-            outs.append(jnp.dot(probs, keys[:, :LATENT], preferred_element_type=f32))
+            outs.append(lax.dot_general(
+                probs, keys[:LATENT], (((1,), (1,)), ((), ())), preferred_element_type=f32))
             lane = lax.broadcasted_iota(jnp.int32, (rows, 128), 1)
             stats.append(jnp.where(lane == 0, top, total))
         return jnp.concatenate(outs, axis=0), jnp.concatenate(stats, axis=0)
 
+    cache_copy.wait()
     own_o, own_s = block(q_ref[...])
     o_copies, s_copies = [], []
     for d in range(1, n):
@@ -130,7 +131,8 @@
 
     part = LATENT // nr
     for k in range(nr):
-        a_send[k] = attended[:, k * part:(k + 1) * part]
+        for r in range(all_rows // heads):
+            a_send[k, r] = attended[r * heads:(r + 1) * heads, k * part:(k + 1) * part]
     copies = []
     for d in range(1, nr):
         k, device = fpeer(d)
@@ -144,14 +146,20 @@
         remote(a_send.at[k], out_ref.at[k], sems.at[6, d], sems.at[7, d], device).wait_recv()
 
 
-def layer_kernel(n, n_role, n_seq, pv_ref, res_ref, gain_ref, wo_hbm, wg_hbm, wu_hbm, wd_hbm,
-                 out_ref, wo, wg, wu, wd, pv_recv, v_send, v_all, v_full, acc, po_send, po_recv,
-                 resid, xg_ref, g_acc, u_acc, gu_send, gu_recv, ss_send, ss_recv, h_send, h_all,
-                 h_full, dn, dn_send, dn_recv, wsem, sems):
+def layer_kernel(n, n_role, n_seq, q_ref, cache_hbm, len_ref, pos_ref, vu_hbm, res_ref, gain_ref,
+                 wo_hbm, wg_hbm, wu_hbm, wd_hbm,
+                 out_ref, cache, vu, q_all, o_send, o_recv, s_send, s_recv, a_send, a_all, a_head,
+                 mixed, pv_ref, wo, wg, wu, wd, pv_recv, v_send, v_all, v_full, acc, po_send,
+                 po_recv, resid, xg_ref, g_acc, u_acc, gu_send, gu_recv, ss_send, ss_recv, h_send,
+                 h_all, h_full, dn, dn_send, dn_recv, wsem, lsem, asems, sems):
     nr = n_role * n_seq
     me, peer = ctx_group(n)
     fme, fpeer = feature_group(n_role, n_seq)
 
+    cache_copy = pltpu.make_async_copy(cache_hbm, cache, lsem.at[0])
+    cache_copy.start()
+    vu_copy = pltpu.make_async_copy(vu_hbm, vu, lsem.at[1])
+    vu_copy.start()
     weights = []
     for which, (hbm, vmem) in enumerate(((wo_hbm, wo), (wg_hbm, wg), (wu_hbm, wu), (wd_hbm, wd))):
         depth = vmem.shape[1]
@@ -165,21 +173,36 @@
         for i in range(vmem.shape[0]):
             fetch(i).start()
     enter(((n, peer), (nr, fpeer)))
-
-    def matmul(x_ref, which, acc_ref):
-        fetch, vmem = weights[which]
-        depth = vmem.shape[1]
-        acc_ref[...] = jnp.zeros_like(acc_ref)
-        if vmem.shape[0] == 1:
+    attend(n, n_role, n_seq, q_ref, cache, cache_copy, len_ref, pos_ref, a_all,
+           q_all, o_send, o_recv, s_send, s_recv, a_send, asems)
+    rows, heads = a_all.shape[1:3]
+    for j in range(nr):
+        for r in range(rows):
+            a_head[:, j * rows + r, :] = a_all[j, r].astype(f32)
+    vu_copy.wait()
+    vdim = vu.shape[2]
+    for h in range(heads):
+        mixed[:, h * vdim:(h + 1) * vdim] = jnp.dot(
+            a_head[h].astype(bf16), vu[h], preferred_element_type=f32)
+    for k in range(nr):
+        pv_ref[k] = mixed[k * rows:(k + 1) * rows, :].astype(bf16)
+
+    def matmul(x_ref, *pairs):
+        chunks, depth, _ = weights[pairs[0][0]][1].shape
+        for which, acc_ref in pairs:
+            fetch, vmem = weights[which]
             fetch(0).wait()
-            acc_ref[...] = jnp.dot(x_ref[...], vmem[0], preferred_element_type=f32)
+            acc_ref[...] = jnp.dot(x_ref[:, :depth], vmem[0], preferred_element_type=f32)
+        if chunks == 1:
             return
 
-        @pl.loop(0, vmem.shape[0])
+        @pl.loop(1, chunks)
         def _(i):
-            fetch(i).wait()
             x = x_ref[:, pl.ds(pl.multiple_of(i * depth, depth), depth)]
-            acc_ref[...] += jnp.dot(x, vmem[i], preferred_element_type=f32)
+            for which, acc_ref in pairs:
+                fetch, vmem = weights[which]
+                fetch(i).wait()
+                acc_ref[...] += jnp.dot(x, vmem[i], preferred_element_type=f32)
 
     def swap(size, peer_of, chunk, recv, row):
         copies = []
@@ -215,7 +238,7 @@
         v_full[k * part:(k + 1) * part, :] = acc_rows
     x_ref = xg_ref[0]
     x_ref[...] = v_full[...].astype(bf16)
-    matmul(x_ref, 0, acc)
+    matmul(x_ref, (0, acc))
 
     po_send[...] = acc[...].astype(bf16)
     copies = swap(n, peer, lambda k: po_send, po_recv, 4)
@@ -233,8 +256,7 @@
     s_copies = swap(nr, fpeer, lambda k: ss_send.at[k], ss_recv, 6)
     x_ref = xg_ref[1]
     x_ref[...] = (total * gain_ref[...]).astype(bf16)
-    matmul(x_ref, 1, g_acc)
-    matmul(x_ref, 2, u_acc)
+    matmul(x_ref, (1, g_acc), (2, u_acc))
 
     for j, a in enumerate((g_acc, u_acc)):
         for k in range(nr):
@@ -259,7 +281,7 @@
         h_full[k * part:(k + 1) * part, :] = h_all[k].astype(f32)
     x_ref = xg_ref[2]
     x_ref[...] = h_full[...].astype(bf16)
-    matmul(x_ref, 3, acc)
+    matmul(x_ref, (3, acc))
 
     for k in range(n):
         piece = acc[k * crows:(k + 1) * crows, :]
@@ -274,7 +296,7 @@
 
 
 def chunk_of(depth):
-    for size in (512, 256):
+    for size in (1024, 768, 512, 256):
         if depth % size == 0:
             return size
     return depth
@@ -292,29 +314,7 @@
     hbm = pl.BlockSpec(memory_space=pl.ANY)
     most = max(n, nr)
     sems = lambda k: pltpu.SemaphoreType.DMA((k, most))
-    attended = pl.pallas_call(
-        functools.partial(attend_kernel, n, n_role, n_seq),
-        out_shape=jax.ShapeDtypeStruct((nr, flat, lat), bf16),
-        in_specs=[vmem, vmem, smem, smem],
-        out_specs=vmem,
-        scratch_shapes=[
-            pltpu.VMEM((n, flat, width), bf16),
-            pltpu.VMEM((n, flat, LATENT), bf16),
-            pltpu.VMEM((n, flat, LATENT), bf16),
-            pltpu.VMEM((n, 8, flat), f32),
-            pltpu.VMEM((n, 8, flat), f32),
-            pltpu.VMEM((nr, flat, lat), bf16),
-            sems(8),
-        ],
-        compiler_params=pltpu.CompilerParams(
-            collective_id=0, has_side_effects=True, vmem_limit_bytes=VMEM_BYTES),
-        name="attend",
-    )(queries.reshape(flat, width), cache, lengths, positions)
-    by_head = attended.reshape(nr, rows, heads, lat).transpose(2, 0, 1, 3).reshape(heads, nr * rows, lat)
-    mixed = jnp.einsum("hrk,hkv->rhv", by_head, value_up_weight, preferred_element_type=f32)
     vwide = heads * value_up_weight.shape[2]
-    pv = mixed.astype(bf16).reshape(nr, rows, vwide)
-
     all_rows, dd = residual.shape
     ff = gate_weight.shape[1]
     part, crows = all_rows // nr, all_rows // n
@@ -329,9 +329,21 @@
     return pl.pallas_call(
         functools.partial(layer_kernel, n, n_role, n_seq),
         out_shape=jax.ShapeDtypeStruct((crows, dd), bf16),
-        in_specs=[vmem] * 3 + [hbm] * 4,
+        in_specs=[vmem, hbm, smem, smem, hbm, vmem, vmem] + [hbm] * 4,
         out_specs=vmem,
         scratch_shapes=[
+            V((cache.shape[0], width, cache.shape[1]), bf16),
+            V(value_up_weight.shape, bf16),
+            V((n, flat, width), bf16),
+            V((n, flat, LATENT), bf16),
+            V((n, flat, LATENT), bf16),
+            V((n, 8, flat), f32),
+            V((n, 8, flat), f32),
+            V((nr, rows, heads, lat), bf16),
+            V((nr, rows, heads, lat), bf16),
+            V((heads, all_rows, lat), f32),
+            V((all_rows, vwide), f32),
+            V((nr, part, vwide), bf16),
             *[held(w) for w in ws],
             V((nr, part, vwide), bf16),
             V((part, vwide), bf16),
@@ -355,12 +367,15 @@
             V((n, crows, dd), bf16),
             V((n, crows, dd), bf16),
             pltpu.SemaphoreType.DMA((4, most_chunks)),
+            pltpu.SemaphoreType.DMA((2,)),
+            sems(8),
             sems(14),
         ],
         compiler_params=pltpu.CompilerParams(
-            collective_id=1, has_side_effects=True, vmem_limit_bytes=VMEM_BYTES),
+            collective_id=0, has_side_effects=True, vmem_limit_bytes=VMEM_BYTES),
         name="layer",
-    )(pv, residual, norm_gain.reshape(1, dd), *ws)
+    )(queries.reshape(flat, width), cache.transpose(0, 2, 1), lengths, positions, value_up_weight,
+      residual, norm_gain.reshape(1, dd), *ws)
 
 
 def solution(mesh):

time: 86.7 us -> 75.9 us (0.88)
  local copies, waits for them, and re-layouts: 8.04 us -> 2.61 us
  Pallas kernels: 78 us -> 73 us
    pallas_call x1 -> x0, Pallas kernels: 42.3 us -> none  [per_device(): pl.pallas_call(functools.partial(attend_kernel, n, n_role, n_seq), out_sh...]
    pallas_call x1, Pallas kernels: 35.6 us -> 73 us  [per_device(): pl.pallas_call(functools.partial(layer_kernel, n, n_role, n_seq), out_sha...]
    unnamed x6 -> x1, local copies, waits for them, and re-layouts: 5.74 us -> 1.32 us
    transpose x1 -> x0, local copies, waits for them, and re-layouts: 0.97 us -> none  [per_device(): attended.reshape(nr, rows, heads, lat).transpose(2, 0, 1, 3)]
where the time goes in v2:
time: 75.9 us; the launch traced here: 75.6 us
  Pallas kernels  73 us (96%)
  local copies, waits for them, and re-layouts  2.61 us (3%)
    pallas_call x1, Pallas kernels, per_device(): pl.pallas_call(functools.partial(layer_kernel, n, n_role, n_seq), out_sha...  73 us

profile of v2, /device:TPU:0, one launch (start us, length us, event | category | flops | bytes accessed | tf_op | source)
XLA Modules:
  0.0 75.6 jit_solution(10489551050571556457)
XLA Ops:
  0.0 1.3 %reshape.7.gain_ref = f32[1,1792]{1,0:T(1,128)} reshape(f32[1792]{0:T(1024)} %param.18) | data formatting | bytes 14336 | tf_op jit(solution)/shard_map/reshape | solution.py:378
  1.3 73.0 %layer.1 = bf16[4,1792]{1,0:T(4,128)(2,1)} custom-call(bf16[128,576]{1,0:T(8,128)(2,1)} %bitcast.3, bf16[2,576,1024]{2,1,0:T(8,128)(2,1)} %bitcast.2, s32[2]{0:T(128)} %len_ref.1, s32[4]{0:T(128)} %pos_ref.1, bf16[32,128,128]{2,1,0:T(8,128)(2,1)} %vu_hbm.1, bf16[16,1792]{1,0:T(8,128)(2,1)} %res_ref.1, f32[1,1792]{1,0:T(1,128)} %reshape.7.gain_ref, ...), custom_call_target="tpu_custom_call" | custom-call | tf_op jit(solution)/shard_map/layer/pallas_call | solution.py:329
  74.3 1.3 %copy.13 = bf16[4,1792]{1,0:T(4,128)(2,1)} copy(bf16[4,1792]{1,0:T(4,128)(2,1)} %layer.1) | data formatting | bytes 28672

commit v3 on v2

--- a/solution.py
+++ b/solution.py
@@ -62,14 +62,16 @@
     me, peer = ctx_group(n)
     fme, fpeer = feature_group(n_role, n_seq)
     seqs, _, context = cache_ref.shape
-    rows = q_ref.shape[0] // seqs
+    rows = q_ref.shape[1]
     heads = rows // MTP
 
     q_copies = []
-    for d in range(1, n):
-        c = remote(q_ref, q_all.at[me], sems.at[0, d], sems.at[1, d], peer(d)[1])
-        c.start()
-        q_copies.append(c)
+    for s in range(seqs):
+        for d in range(1, n):
+            c = remote(q_ref.at[s], q_all.at[me, s], sems.at[s, d], sems.at[seqs + s, d],
+                       peer(d)[1])
+            c.start()
+            q_copies.append(c)
 
     places = me * context + lax.broadcasted_iota(jnp.int32, (rows, context), 1)
     first = lax.broadcasted_iota(jnp.int32, (rows, context), 0) < heads
@@ -78,72 +80,77 @@
         limit = jnp.where(first, pos_ref[MTP * s], pos_ref[MTP * s + 1])
         lives.append((places < len_ref[s]) & (places <= limit))
 
-    def block(q):
-        outs, stats = [], []
-        for s in range(seqs):
-            keys = cache_ref[s]
-            scores = lax.dot_general(
-                q[s * rows:(s + 1) * rows], keys, (((1,), (0,)), ((), ())),
-                preferred_element_type=f32) * softmax_scale
-            live = lives[s]
-            top = jnp.max(jnp.where(live, scores, -1e30), axis=1, keepdims=True)
-            probs = jnp.exp(jnp.where(live, scores - top, -1e30)).astype(bf16)
-            total = jnp.sum(probs.astype(f32), axis=1, keepdims=True)
-            outs.append(lax.dot_general(
-                probs, keys[:LATENT], (((1,), (1,)), ((), ())), preferred_element_type=f32))
-            lane = lax.broadcasted_iota(jnp.int32, (rows, 128), 1)
-            stats.append(jnp.where(lane == 0, top, total))
-        return jnp.concatenate(outs, axis=0), jnp.concatenate(stats, axis=0)
+    lane = lax.broadcasted_iota(jnp.int32, (rows, 128), 1)
+
+    def block(q, s):
+        keys = cache_ref[s]
+        scores = jnp.dot(q, keys, preferred_element_type=f32) * softmax_scale
+        live = lives[s]
+        top = jnp.max(jnp.where(live, scores, -1e30), axis=1, keepdims=True)
+        probs = jnp.exp(jnp.where(live, scores - top, -1e30)).astype(bf16)
+        total = jnp.sum(probs.astype(f32), axis=1, keepdims=True)
+        out = lax.dot_general(
+            probs, keys[:LATENT], (((1,), (1,)), ((), ())), preferred_element_type=f32)
+        return out, top, total
 
     cache_copy.wait()
-    own_o, own_s = block(q_ref[...])
-    o_copies, s_copies = [], []
-    for d in range(1, n):
-        src, device = peer(n - d)
-        remote(q_all.at[src], q_all.at[src], sems.at[0, d], sems.at[1, d], device).wait_recv()
-        o, s = block(q_all[src])
-        o_send[d] = o.astype(bf16)
-        s_send[d] = s.T[0:8]
-        c = remote(o_send.at[d], o_recv.at[d], sems.at[2, d], sems.at[3, d], device)
-        c.start()
-        o_copies.append(c)
-        c = remote(s_send.at[d], s_recv.at[d], sems.at[4, d], sems.at[5, d], device)
-        c.start()
-        s_copies.append(c)
+    own = [block(q_ref[s], s) for s in range(seqs)]
+    o_copies, s_copies = {}, {}
+    for s in range(seqs):
+        for d in range(1, n):
+            src, device = peer(n - d)
+            remote(q_ref.at[s], q_all.at[src, s], sems.at[s, d], sems.at[seqs + s, d],
+                   device).wait_recv()
+            o, top, total = block(q_all[src, s], s)
+            o_send[d, s] = o.astype(bf16)
+            s_send[d, s] = jnp.where(lane == 0, top, total).T[0:8]
+            c = remote(o_send.at[d, s], o_recv.at[d, s], sems.at[2 * seqs + s, d],
+                       sems.at[3 * seqs + s, d], device)
+            c.start()
+            o_copies[s, d] = c
+            c = remote(s_send.at[d, s], s_recv.at[d, s], sems.at[4 * seqs + s, d],
+                       sems.at[5 * seqs + s, d], device)
+            c.start()
+            s_copies[s, d] = c
     for c in q_copies:
         c.wait_send()
 
-    all_rows = q_ref.shape[0]
-    tops, totals = [own_s[:, 0:1]], [own_s[:, 1:2]]
-    for d in range(1, n):
-        s_copies[d - 1].wait()
-        back = jnp.concatenate([s_recv[d]] * 16, axis=0).T
-        tops.append(back[:, 0:1])
-        totals.append(back[:, 1:2])
-    highest = functools.reduce(jnp.maximum, tops)
-    factors = [jnp.exp(t - highest) for t in tops]
-    denom = sum(f * t for f, t in zip(factors, totals))
-    numer = factors[0] * own_o
-    for d in range(1, n):
-        o_copies[d - 1].wait()
-        numer = numer + factors[d] * o_recv[d].astype(f32)
-    attended = (numer / denom).astype(bf16)
+    heads = rows // MTP
+    merged = []
+    for s in range(seqs):
+        own_o, top, total = own[s]
+        tops, totals = [top], [total]
+        for d in range(1, n):
+            s_copies[s, d].wait()
+            back = jnp.concatenate([s_recv[d, s]] * 16, axis=0).T
+            tops.append(back[:, 0:1])
+            totals.append(back[:, 1:2])
+        highest = functools.reduce(jnp.maximum, tops)
+        factors = [jnp.exp(t - highest) for t in tops]
+        denom = sum(f * t for f, t in zip(factors, totals))
+        numer = factors[0] * own_o
+        for d in range(1, n):
+            o_copies[s, d].wait()
+            numer = numer + factors[d] * o_recv[d, s].astype(f32)
+        merged.append((numer / denom).astype(bf16))
 
     part = LATENT // nr
     for k in range(nr):
-        for r in range(all_rows // heads):
-            a_send[k, r] = attended[r * heads:(r + 1) * heads, k * part:(k + 1) * part]
+        for r in range(seqs * MTP):
+            t = r % MTP
+            a_send[k, r] = merged[r // MTP][t * heads:(t + 1) * heads, k * part:(k + 1) * part]
     copies = []
     for d in range(1, nr):
         k, device = fpeer(d)
-        c = remote(a_send.at[k], out_ref.at[fme], sems.at[6, d], sems.at[7, d], device)
+        c = remote(a_send.at[k], out_ref.at[fme], sems.at[6 * seqs, d], sems.at[7 * seqs, d], device)
         c.start()
         copies.append(c)
     out_ref[fme] = a_send[fme]
     for d in range(1, nr):
         k, device = fpeer(nr - d)
         copies[d - 1].wait_send()
-        remote(a_send.at[k], out_ref.at[k], sems.at[6, d], sems.at[7, d], device).wait_recv()
+        remote(a_send.at[k], out_ref.at[k], sems.at[6 * seqs, d], sems.at[7 * seqs, d],
+               device).wait_recv()
 
 
 def layer_kernel(n, n_role, n_seq, q_ref, cache_hbm, len_ref, pos_ref, vu_hbm, res_ref, gain_ref,
@@ -307,7 +314,8 @@
     n, n_role, n_seq = sizes
     nr = n_role * n_seq
     rows, heads, width = queries.shape
-    flat = rows * heads
+    seqs = cache.shape[0]
+    span = rows * heads // seqs
     lat = LATENT // nr
     vmem = pl.BlockSpec(memory_space=pltpu.VMEM)
     smem = pl.BlockSpec(memory_space=pltpu.SMEM)
@@ -334,11 +342,11 @@
         scratch_shapes=[
             V((cache.shape[0], width, cache.shape[1]), bf16),
             V(value_up_weight.shape, bf16),
-            V((n, flat, width), bf16),
-            V((n, flat, LATENT), bf16),
-            V((n, flat, LATENT), bf16),
-            V((n, 8, flat), f32),
-            V((n, 8, flat), f32),
+            V((n, seqs, span, width), bf16),
+            V((n, seqs, span, LATENT), bf16),
+            V((n, seqs, span, LATENT), bf16),
+            V((n, seqs, 8, span), f32),
+            V((n, seqs, 8, span), f32),
             V((nr, rows, heads, lat), bf16),
             V((nr, rows, heads, lat), bf16),
             V((heads, all_rows, lat), f32),
@@ -368,13 +376,13 @@
             V((n, crows, dd), bf16),
             pltpu.SemaphoreType.DMA((4, most_chunks)),
             pltpu.SemaphoreType.DMA((2,)),
-            sems(8),
+            sems(8 * seqs),
             sems(14),
         ],
         compiler_params=pltpu.CompilerParams(
             collective_id=0, has_side_effects=True, vmem_limit_bytes=VMEM_BYTES),
         name="layer",
-    )(queries.reshape(flat, width), cache.transpose(0, 2, 1), lengths, positions, value_up_weight,
+    )(queries.reshape(seqs, span, width), cache.transpose(0, 2, 1), lengths, positions, value_up_weight,
       residual, norm_gain.reshape(1, dd), *ws)
 
 

time: 75.9 us -> 74.1 us (0.976)
  Pallas kernels: 73 us -> 71.2 us
    pallas_call x1, Pallas kernels: 73 us -> 71.2 us  [per_device(): pl.pallas_call(functools.partial(layer_kernel, n, n_role, n_seq), out_sha...]
where the time goes in v3:
time: 74.1 us; the launch traced here: 73.9 us
  Pallas kernels  71.2 us (96%)
  local copies, waits for them, and re-layouts  2.61 us (4%)
    pallas_call x1, Pallas kernels, per_device(): pl.pallas_call(functools.partial(layer_kernel, n, n_role, n_seq), out_sha...  71.2 us

profile of v3, /device:TPU:0, one launch (start us, length us, event | category | flops | bytes accessed | tf_op | source)
XLA Modules:
  0.0 73.9 jit_solution(13575558870737305548)
XLA Ops:
  0.0 1.3 %reshape.7.gain_ref = f32[1,1792]{1,0:T(1,128)} reshape(f32[1792]{0:T(1024)} %param.18) | data formatting | bytes 14336 | tf_op jit(solution)/shard_map/reshape | solution.py:386
  1.3 71.2 %layer.1 = bf16[4,1792]{1,0:T(4,128)(2,1)} custom-call(bf16[2,64,576]{2,1,0:T(8,128)(2,1)} %bitcast.3, bf16[2,576,1024]{2,1,0:T(8,128)(2,1)} %bitcast.2, s32[2]{0:T(128)} %len_ref.1, s32[4]{0:T(128)} %pos_ref.1, bf16[32,128,128]{2,1,0:T(8,128)(2,1)} %vu_hbm.1, bf16[16,1792]{1,0:T(8,128)(2,1)} %res_ref.1, f32[1,1792]{1,0:T(1,128)} %reshape.7.gain_ref, ...), custom_call_target="tpu_custom_call" | custom-call | tf_op jit(solution)/shard_map/layer/pallas_call | solution.py:337
  72.5 1.3 %copy.13 = bf16[4,1792]{1,0:T(4,128)(2,1)} copy(bf16[4,1792]{1,0:T(4,128)(2,1)} %layer.1) | data formatting | bytes 28672
